TPU v7x, 32 devices: a whole 2x2x4 slice. The times are simulated.
32 devices in a mesh: dp: 2 (over x), ep: 16 (over y, z, core).
Axes of the slice: x: 2, y: 2, z: 4, core: 2. Of those that a mesh axis runs over, the one named last changes fastest.
Arguments:
- x: bfloat16 [2, 16, 256, 1536], P('dp', 'ep'), parts along dimension 0
- expert: int32 [2, 16, 256, 2], P('dp', 'ep'), parts along dimension 0
- slot: int32 [2, 16, 256, 2], P('dp', 'ep'), parts along dimension 0
- gate: float32 [2, 16, 256, 2], P('dp', 'ep'), parts along dimension 0
- w_gate: bfloat16 [32, 1536, 9216], P('ep')
- w_up: bfloat16 [32, 1536, 9216], P('ep')
- w_down: bfloat16 [32, 9216, 1536], P('ep')
Outputs:
- y: bfloat16 [2, 16, 256, 1536], P('dp', 'ep'), parts along dimension 0
There are 2 independent parts. A program takes and returns all parts, laid end to end along the dimension named above; an argument that names none is the same for every part.
All inputs are finite; a program needn't handle non-finite values.
Results may differ from a plain program's by a relative error of at most 0.009.
Values are sent between devices in bfloat16 or wider.
A program may use at most 2 GiB of HBM per device.

v0:
```python
import jax
import jax.numpy as jnp
from jax import lax
from jax.sharding import NamedSharding, PartitionSpec as P


def einsum(form, a, b):
    return jnp.einsum(form, a.astype(jnp.float32), b.astype(jnp.float32))


def solution(mesh):
    def placed(v, *spec):
        return lax.with_sharding_constraint(v, NamedSharding(mesh, P(*spec)))

    def step(x, expert, slot, gate, w_gate, w_up, w_down):
        experts, (tokens, top) = w_gate.shape[0], expert.shape[2:]
        slots = 5 * tokens * top // (4 * experts)
        to_expert = jax.nn.one_hot(expert, experts, dtype=jnp.bfloat16)
        to_slot = jax.nn.one_hot(slot, slots, dtype=jnp.bfloat16)
        weighted = to_expert * gate[..., None].astype(jnp.bfloat16)
        dispatch = einsum("abtke,abtkc->abtec", to_expert, to_slot).astype(jnp.bfloat16)
        combine = einsum("abtke,abtkc->abtec", weighted, to_slot).astype(jnp.bfloat16)
        z = einsum("abtec,abtd->aebcd", dispatch, x).astype(jnp.bfloat16)
        z = placed(z, "dp", None, "ep", None, None)
        z = placed(z, "dp", "ep", None, None, None)
        h = jax.nn.silu(einsum("aebcd,edf->aebcf", z, w_gate))
        h = (h * einsum("aebcd,edf->aebcf", z, w_up)).astype(jnp.bfloat16)
        out = einsum("aebcf,efd->aebcd", h, w_down).astype(jnp.bfloat16)
        out = placed(out, "dp", "ep", None, None, None)
        out = placed(out, "dp", None, "ep", None, None)
        y = einsum("abtec,aebcd->abtd", combine, out)
        return y.astype(jnp.bfloat16)

    return step
```

profile of v0, /device:TPU:0, one launch (start us, length us, event | category | flops | bytes accessed | tf_op | source)
XLA Modules:
  0.0 237.9 jit_solution(14464529595874538454)
XLA Ops:
  0.0 0.0 copy-start
  0.0 0.9 copy.11
  0.9 0.0 copy-start.2
  0.9 0.8 copy.9
  1.8 0.6 copy-done.4
  2.4 2.8 %convolution_convert_fusion.1 = bf16[256,32,20]{1,2,0:T(8,128)(2,1)S(1)} fusion(s32[256,2]{1,0:T(8,128)S(1)} %copy.11, s32[256,2]{1,0:T(8,128)S(1)} %copy.9), kind=kOutput, calls=%fused_computation.25 | convolution fusion | flops 845824 | bytes 331776 | tf_op jit(solution)/abtke,abtkc->abtec/dot_general | solution.py:8
  5.2 0.0 copy-done
  5.2 0.9 convolution_convert_fusion
  6.1 1.8 reshape.6
  7.9 2.9 %copy.13 = bf16[1,16,2,1,20,1536]{5,2,4,3,0,1:T(2,128)(2,1)S(1)} copy(bf16[1,16,2,1,20,1536]{5,2,1,4,3,0:T(2,128)(2,1)} %reshape.6) | data formatting | bytes 3932160 | tf_op jit(solution)/sharding_constraint;jit(solution)/sharding_constraint | solution.py:13
  10.8 52.2 %all-to-all.4 = bf16[1,16,2,1,20,1536]{5,2,4,3,0,1:T(2,128)(2,1)S(1)} all-to-all(bf16[1,16,2,1,20,1536]{5,2,4,3,0,1:T(2,128)(2,1)S(1)} %copy.13), channel_id=1, replica_groups=mesh['dp'=2,'ep'=16] {'ep'}, dimensions={1} | all-to-all | bytes 3932160 | tf_op jit(solution)/sharding_constraint;jit(solution)/sharding_constraint | solution.py:13
  63.0 34.9 %fusion.4 = f32[2,16,20,9216]{3,2,1,0:T(8,128)} fusion(bf16[2,1536,9216]{2,1,0:T(8,128)(2,1)} %param.4, bf16[1,16,2,1,20,1536]{5,2,4,3,0,1:T(2,128)(2,1)S(1)} %all-to-all.4), kind=kOutput, calls=%fused_computation.4 | convolution fusion | flops 18119393280 | bytes 82182144 | tf_op jit(solution)/aebcd,edf->aebcf/dot_general | solution.py:8
  97.8 44.4 %fusion.67 = bf16[2,16,20,9216]{3,2,1,0:T(8,128)(2,1)} fusion(bf16[2,1536,9216]{2,1,0:T(8,128)(2,1)} %param.5, f32[2,16,20,9216]{3,2,1,0:T(8,128)} %fusion.4, bf16[1,16,2,1,20,1536]{5,2,4,3,0,1:T(2,128)(2,1)S(1)} %all-to-all.4), kind=kOutput, calls=%fused_computation.13.clone.clone.clone.clone.clone.1 | convolution fusion | flops 18154782720 | bytes 93978624 | tf_op jit(solution)/aebcd,edf->aebcf/dot_general | solution.py:8
  142.3 30.8 %fusion.25 = bf16[1,2,16,1,20,1536]{5,4,2,1,3,0:T(8,128)(2,1)S(1)} fusion(bf16[2,9216,1536]{2,1,0:T(8,128)(2,1)} %param.6, bf16[2,16,20,9216]{3,2,1,0:T(8,128)(2,1)} %fusion.67), kind=kOutput, calls=%fused_computation.17 | convolution fusion | flops 18120376320 | bytes 70385664 | tf_op jit(solution)/aebcf,efd->aebcd/dot_general | solution.py:8
  173.1 3.3 %copy.15 = bf16[1,2,16,1,20,1536]{5,1,4,3,0,2:T(2,128)(2,1)} copy(bf16[1,2,16,1,20,1536]{5,4,2,1,3,0:T(8,128)(2,1)S(1)} %fusion.25) | data formatting | bytes 3932160 | tf_op jit(solution)/sharding_constraint;jit(solution)/sharding_constraint | solution.py:13
  176.4 7.0 %all-to-all-start.1 = ((bf16[1,2,16,1,20,1536]{5,1,4,3,0,2:T(2,128)(2,1)}), bf16[1,2,16,1,20,1536]{5,1,4,3,0,2:T(2,128)(2,1)S(1)}, u32[]{:S(2)}, u32[]{:S(2)}) async-start(bf16[1,2,16,1,20,1536]{5,1,4,3,0,2:T(2,128)(2,1)} %copy.15), calls=%async_computation.1 | async-start | bytes 3932160 | tf_op jit(solution)/sharding_constraint;jit(solution)/sharding_constraint | solution.py:13
  183.5 0.1 copy.10
  183.6 0.0 copy-done.3
  183.6 3.9 %convolution_convert_fusion.2 = bf16[256,32,20]{1,2,0:T(8,128)(2,1)} fusion(s32[256,2]{1,0:T(8,128)S(1)} %copy-done.3, s32[256,2]{1,0:T(8,128)S(1)} %copy-done.5, bf16[256,2]{1,0:T(8,128)(2,1)S(1)} %copy.10), kind=kOutput, calls=%fused_computation.26 | convolution fusion | flops 862208 | bytes 332800 | tf_op jit(solution)/abtke,abtkc->abtec/dot_general | solution.py:8
  187.5 39.4 %all-to-all-done.1 = bf16[1,2,16,1,20,1536]{5,1,4,3,0,2:T(2,128)(2,1)S(1)} async-done(((bf16[1,2,16,1,20,1536]{5,1,4,3,0,2:T(2,128)(2,1)}), bf16[1,2,16,1,20,1536]{5,1,4,3,0,2:T(2,128)(2,1)S(1)}, u32[]{:S(2)}, u32[]{:S(2)}) %all-to-all-start.1) | async-done | bytes 1966112 | tf_op jit(solution)/sharding_constraint;jit(solution)/sharding_constraint | solution.py:13
  226.9 3.3 %copy.16 = bf16[1,16,2,1,20,1536]{5,2,1,4,3,0:T(2,128)(2,1)} copy(bf16[1,16,2,1,20,1536]{5,2,4,3,0,1:T(2,128)(2,1)S(1)} %bitcast.131) | data formatting | bytes 3932160 | tf_op jit(solution)/sharding_constraint;jit(solution)/sharding_constraint | solution.py:13
  230.2 4.3 %reshape.46 = bf16[32,20,1536]{2,0,1:T(8,128)(2,1)S(1)} reshape(bf16[1,16,2,1,20,1536]{5,2,1,4,3,0:T(2,128)(2,1)} %copy.16) | data formatting | bytes 3932160
  234.5 0.0 copy-start.1
  234.5 3.4 %fusion.33 = bf16[1,1,256,1536]{3,2,1,0:T(8,128)(2,1)} fusion(bf16[32,20,1536]{2,0,1:T(8,128)(2,1)S(1)} %reshape.46, bf16[256,32,20]{1,2,0:T(8,128)(2,1)} %convolution_convert_fusion.2), kind=kOutput, calls=%fused_computation.20 | convolution fusion | flops 503709696 | bytes 3080192 | tf_op jit(solution)/abtec,aebcd->abtd/dot_general | solution.py:8
  (9 shorter events, 0.0 us)
Async XLA Ops:
  0.0 5.2 %copy-start = (bf16[1,1,256,1536]{3,2,1,0:T(8,128)(2,1)S(1)}, bf16[1,1,256,1536]{3,2,1,0:T(8,128)(2,1)}, u32[]{:S(2)}) copy-start(bf16[1,1,256,1536]{3,2,1,0:T(8,128)(2,1)} %param.3) | copy-start | bytes 2359300
  0.9 0.9 copy-start.2
  1.8 0.7 copy-start.4
  176.4 7.0 %copy-start.6 = (f32[1,1,256,2]{2,3,1,0:T(2,128)S(1)}, f32[1,1,256,2]{2,3,1,0:T(2,128)}, u32[]{:S(2)}) copy-start(f32[1,1,256,2]{2,3,1,0:T(2,128)} %param.1) | copy-start | bytes 6148
  176.4 7.2 %copy-start.3 = (s32[256,2]{1,0:T(8,128)S(1)}, s32[256,2]{1,0:T(8,128)}, u32[]{:S(2)}) copy-start(s32[256,2]{1,0:T(8,128)} %copy-done.2) | copy-start | bytes 6148
  176.4 7.2 %copy-start.5 = (s32[256,2]{1,0:T(8,128)S(1)}, s32[256,2]{1,0:T(8,128)}, u32[]{:S(2)}) copy-start(s32[256,2]{1,0:T(8,128)} %copy-done.4) | copy-start | bytes 6148
  176.4 50.5 %all-to-all-start.1 = ((bf16[1,2,16,1,20,1536]{5,1,4,3,0,2:T(2,128)(2,1)}), bf16[1,2,16,1,20,1536]{5,1,4,3,0,2:T(2,128)(2,1)S(1)}, u32[]{:S(2)}, u32[]{:S(2)}) async-start(bf16[1,2,16,1,20,1536]{5,1,4,3,0,2:T(2,128)(2,1)} %copy.15), calls=%async_computation.1 | async-start | bytes 3932160 | tf_op jit(solution)/sharding_constraint;jit(solution)/sharding_constraint | solution.py:13
  234.5 3.4 %copy-start.1 = (bf16[1,1,256,1536]{3,2,1,0:T(8,128)(2,1)S(1)}, bf16[1,1,256,1536]{3,2,1,0:T(8,128)(2,1)}, u32[]{:S(2)}) copy-start(bf16[1,1,256,1536]{3,2,1,0:T(8,128)(2,1)} %param.3) | copy-start | bytes 2359300
where the time goes:
time: 239 us; the launch traced here: 238 us
  matrix products  121 us (51%)
  blocking collectives  52.2 us (22%)
  waiting for transfers between devices  39.4 us (16%)
  local copies, waits for them, and re-layouts  18.1 us (8%)
  starting transfers between devices  7.01 us (3%)
    dot_general x7, matrix products, einsum(): return jnp.einsum(form, a.astype(jnp.float32), b.astype(jnp.float32))  121 us
    another operation x1, blocking collectives, placed(): return lax.with_sharding_constraint(v, NamedSharding(mesh, P(*spec)))  52.2 us
    another operation x1, waiting for transfers between devices, placed(): return lax.with_sharding_constraint(v, NamedSharding(mesh, P(*spec)))  39.4 us
    another operation x4, local copies, waits for them, and re-layouts, placed(): return lax.with_sharding_constraint(v, NamedSharding(mesh, P(*spec)))  11.3 us
    another operation x1, starting transfers between devices, placed(): return lax.with_sharding_constraint(v, NamedSharding(mesh, P(*spec)))  7.01 us
    unnamed x17, local copies, waits for them, and re-layouts  6.66 us
  transfers between devices with their start and end apart: 1, of which 1 were waited for; matrix products, arithmetic and copies ran while one was open for 2% of the time, Pallas kernels for 0%

commit v1 on v0

v1 whole, which is shorter than its diff:
```python
import functools

import jax
import jax.numpy as jnp
from jax import lax
from jax.experimental import pallas as pl
from jax.experimental.pallas import tpu as pltpu
from jax.sharding import PartitionSpec as P

MESH = pl.DeviceIdType.MESH
N = 16
C = 20
T, D, F = 256, 1536, 9216
HD = D // 2
QD = HD // 2
NBUF = 4
TF = 1024
NJ = F // TF
OC = 512
NC = D // OC
NK = 3
PER = 2 * NJ + NC * NK
STEPS = 2 * PER
ROWS = N * C


def swap(a, b, first):
    return jnp.where(first, a, pltpu.roll(b, C, 0)), jnp.where(first, pltpu.roll(a, C, 0), b)


def peer(me, k):
    y, z, c = me // 8, (me // 2) % 4, me % 2
    half = (z // 2 + (k // 8) + 1) % 2
    zz = half * 2 + (z + k // 2) % 2
    return ((y + (k // 4)) % 2) * 8 + zz * 2 + (c + k) % 2


def kernel(
    expert_ref, slot_ref, gate_ref, x_ref, wg, wu, wd, y_ref,
    send, recv, rsend, rrecv, zbuf, zl, acc, h, oacc, obuf, ct, wbuf,
    wsem, ssem, rsem, rssem, rrsem,
):
    dp, me = lax.axis_index("dp"), lax.axis_index("ep")

    def fetch(n):
        s = n % NBUF
        e, r = n // PER, n % PER

        @pl.when(r < 2 * NJ)
        def _():
            hf, j = r // NJ, r % NJ
            rows = pl.ds(hf * HD, HD)
            for q in range(4):
                w = wg if q < 2 else wu
                cols = pl.ds(j * TF + (q % 2) * 512, 512)
                pltpu.make_async_copy(w.at[e, rows, cols], wbuf.at[s, q], wsem.at[s, q]).start()

        @pl.when(r >= 2 * NJ)
        def _():
            c, k = (r - 2 * NJ) // NK, (r - 2 * NJ) % NK
            for q in range(4):
                rows = pl.ds(k * 4 * HD + q * HD, HD)
                cols = pl.ds(c * OC, OC)
                pltpu.make_async_copy(wd.at[e, rows, cols], wbuf.at[s, q], wsem.at[s, q]).start()

    def arrived(n):
        s = n % NBUF
        for q in range(4):
            pltpu.make_async_copy(wg.at[0, pl.ds(0, HD), pl.ds(0, 512)], wbuf.at[s, q], wsem.at[s, q]).wait()
        return s

    def refill(n):
        @pl.when(n + NBUF < STEPS)
        def _():
            fetch(n + NBUF)

    barrier = pltpu.get_barrier_semaphore()

    @pl.loop(1, N)
    def _(k):
        pl.semaphore_signal(barrier, inc=1, device_id=(dp, (me + k) % N), device_id_type=MESH)

    @pl.loop(0, NBUF)
    def _(n):
        fetch(n)

    key = jnp.where(slot_ref[...] < C, expert_ref[...] * C + slot_ref[...], -1)
    k0, k1 = key[0:1, :], key[1:2, :]
    gate = gate_ref[...].astype(jnp.bfloat16).astype(jnp.float32)
    row = lax.broadcasted_iota(jnp.int32, (2 * ROWS, T), 0)
    hit0, hit1 = k0 == row, k1 == row
    pick = (jnp.where(hit0, 1.0, 0.0) + jnp.where(hit1, 1.0, 0.0)).astype(jnp.bfloat16)
    weighted = jnp.where(hit0, gate[0:1, :], 0.0) + jnp.where(hit1, gate[1:2, :], 0.0)
    ct[...] = weighted.astype(jnp.bfloat16)
    first_q = lax.broadcasted_iota(jnp.int32, (2 * C, QD), 0) < C
    first_o = lax.broadcasted_iota(jnp.int32, (2 * C, OC // 2), 0) < C

    def dispatch(e, hf, k):
        to = peer(me, k)
        return pltpu.make_async_remote_copy(
            send.at[e, hf, to], recv.at[e, hf, me], ssem.at[e, hf, to], rsem.at[e, hf, me],
            device_id=(dp, to), device_id_type=MESH,
        )

    def send_all(e, hf):
        @pl.loop(0, N - 1)
        def _(i):
            dispatch(e, hf, i + i // 8).start()

        recv[e, hf, me] = send[e, hf, me]

    for hf in range(2):
        zbuf[...] = jnp.dot(pick, x_ref[:, hf * HD : (hf + 1) * HD], preferred_element_type=jnp.float32)

        @pl.loop(0, N)
        def _(d):
            rows = pl.ds(pl.multiple_of(d * 2 * C, 8), 2 * C)
            a, b = swap(zbuf[rows, :QD], zbuf[rows, QD:], first_q)
            send[0, hf, d] = a.astype(jnp.bfloat16)
            send[1, hf, d] = b.astype(jnp.bfloat16)

        if hf == 0:
            pl.semaphore_wait(barrier, N - 1)
        send_all(0, hf)
    send_all(1, 0)
    send_all(1, 1)

    def gathered(e, hf):
        @pl.loop(0, N - 1)
        def _(i):
            src = (me + 1 + i) % N
            pltpu.make_async_remote_copy(
                send.at[e, hf, src], recv.at[e, hf, src], ssem.at[e, hf, src], rsem.at[e, hf, src],
                device_id=(dp, src), device_id_type=MESH,
            ).wait_recv()

        @pl.loop(0, N // 4)
        def _(p):
            blocks = [recv[e, hf, 4 * p + i].astype(jnp.float32) for i in range(4)]
            l0, h0 = swap(blocks[0], blocks[1], first_q)
            l1, h1 = swap(blocks[2], blocks[3], first_q)
            rows = pl.ds(pl.multiple_of(p * 4 * C, 16), 4 * C)
            zl[rows, :QD] = jnp.concatenate([l0, l1], axis=0).astype(jnp.bfloat16)
            zl[rows, QD:] = jnp.concatenate([h0, h1], axis=0).astype(jnp.bfloat16)

    def back(e, c, k):
        to = peer(me, k)
        return pltpu.make_async_remote_copy(
            rsend.at[e, c, to], rrecv.at[e, c, me], rssem.at[e, c, to], rrsem.at[e, c, me],
            device_id=(dp, to), device_id_type=MESH,
        )

    dot = functools.partial(jnp.dot, preferred_element_type=jnp.float32)

    @pl.loop(0, 2)
    def _(e):
        gathered(e, 0)

        @pl.loop(0, NJ)
        def _(j):
            n = e * PER + j
            s = arrived(n)
            for q in range(4):
                acc[j, q] = dot(zl[...], wbuf[s, q])
            refill(n)

        gathered(e, 1)

        @pl.loop(0, NJ)
        def _(j):
            n = e * PER + NJ + j
            s = arrived(n)
            for q in range(2):
                g = acc[j, q] + dot(zl[...], wbuf[s, q])
                u = acc[j, q + 2] + dot(zl[...], wbuf[s, q + 2])
                h[j, q] = (g * jax.nn.sigmoid(g) * u).astype(jnp.bfloat16)
            refill(n)

        @pl.loop(0, NC)
        def _(c):
            @pl.loop(0, NK)
            def _(k):
                n = e * PER + 2 * NJ + c * NK + k
                s = arrived(n)
                total = jnp.zeros((ROWS, OC), jnp.float32)
                for q in range(4):
                    at = [q * HD + o for o in range(0, HD, 256)]
                    left = [h[3 * k + o // TF, o % TF // 512, :, o % 512 : o % 512 + 256] for o in at]
                    total += dot(jnp.concatenate(left, axis=1), wbuf[s, q])

                @pl.when(k == 0)
                def _():
                    oacc[...] = total

                @pl.when(k > 0)
                def _():
                    oacc[...] += total

                refill(n)

            @pl.loop(0, N // 2)
            def _(p):
                rows = pl.ds(pl.multiple_of(p * 2 * C, 8), 2 * C)
                a, b = swap(oacc[rows, : OC // 2], oacc[rows, OC // 2 :], first_o)
                rsend[e, c, 2 * p] = a.astype(jnp.bfloat16)
                rsend[e, c, 2 * p + 1] = b.astype(jnp.bfloat16)

            @pl.loop(0, N - 1)
            def _(i):
                back(e, c, i + i // 8).start()

            rrecv[e, c, me] = rsend[e, c, me]

    for c in range(NC):
        @pl.loop(0, N - 1)
        def _(i):
            src = (me + 1 + i) % N
            for e in range(2):
                pltpu.make_async_remote_copy(
                    rsend.at[e, c, src], rrecv.at[e, c, src], rssem.at[e, c, src], rrsem.at[e, c, src],
                    device_id=(dp, src), device_id_type=MESH,
                ).wait_recv()

        @pl.loop(0, N // 2)
        def _(p):
            parts = [
                swap(rrecv[0, c, 2 * p + i].astype(jnp.float32), rrecv[1, c, 2 * p + i].astype(jnp.float32), first_o)
                for i in range(2)
            ]
            rows = pl.ds(pl.multiple_of(p * 4 * C, 16), 4 * C)
            for i in range(2):
                obuf[rows, i * (OC // 2) : (i + 1) * (OC // 2)] = jnp.concatenate(
                    [parts[0][i], parts[1][i]], axis=0
                ).astype(jnp.bfloat16)

        y_ref[:, c * OC : (c + 1) * OC] = lax.dot_general(
            ct[...], obuf[...], (((0,), (0,)), ((), ())), preferred_element_type=jnp.float32
        ).astype(jnp.bfloat16)

    @pl.loop(0, N - 1)
    def _(i):
        k = i + i // 8
        for e in range(2):
            for hf in range(2):
                dispatch(e, hf, k).wait_send()
            for c in range(NC):
                back(e, c, k).wait_send()


def solution(mesh):
    spec = P("dp", "ep")

    def layer(x, expert, slot, gate, w_gate, w_up, w_down):
        vmem = pl.BlockSpec(memory_space=pltpu.VMEM)
        hbm = pl.BlockSpec(memory_space=pl.ANY)
        bf16, f32 = jnp.bfloat16, jnp.float32
        dma = pltpu.SemaphoreType.DMA
        y = pl.pallas_call(
            kernel,
            out_shape=jax.ShapeDtypeStruct((T, D), bf16),
            in_specs=[vmem] * 4 + [hbm] * 3,
            out_specs=vmem,
            scratch_shapes=[
                pltpu.VMEM((2, 2, N, 2 * C, QD), bf16),
                pltpu.VMEM((2, 2, N, 2 * C, QD), bf16),
                pltpu.VMEM((2, NC, N, 2 * C, OC // 2), bf16),
                pltpu.VMEM((2, NC, N, 2 * C, OC // 2), bf16),
                pltpu.VMEM((2 * ROWS, HD), f32),
                pltpu.VMEM((ROWS, HD), bf16),
                pltpu.VMEM((NJ, 4, ROWS, 512), f32),
                pltpu.VMEM((NJ, 2, ROWS, 512), bf16),
                pltpu.VMEM((ROWS, OC), f32),
                pltpu.VMEM((2 * ROWS, OC), bf16),
                pltpu.VMEM((2 * ROWS, T), bf16),
                pltpu.VMEM((NBUF, 4, HD, 512), bf16),
                dma((NBUF, 4)),
                dma((2, 2, N)),
                dma((2, 2, N)),
                dma((2, NC, N)),
                dma((2, NC, N)),
            ],
            compiler_params=pltpu.CompilerParams(
                collective_id=0, has_side_effects=True, vmem_limit_bytes=66_000_000
            ),
            name="moe",
        )(
            expert.reshape(T, 2).T, slot.reshape(T, 2).T, gate.reshape(T, 2).T,
            x.reshape(T, D), w_gate, w_up, w_down,
        )
        return y.reshape(1, 1, T, D)

    return jax.shard_map(
        layer, mesh=mesh,
        in_specs=(spec, spec, spec, spec, P("ep"), P("ep"), P("ep")),
        out_specs=spec, check_vma=False,
    )
```

time: 239 us -> 124 us (0.52)
  matrix products: 121 us -> 0 us
  Pallas kernels: 0 us -> 121 us
  blocking collectives: 52.2 us -> 0 us
  waiting for transfers between devices: 39.4 us -> 0 us
  local copies, waits for them, and re-layouts: 18.1 us -> 2.06 us
  starting transfers between devices: 7.01 us -> 0 us
    pallas_call x0 -> x1, Pallas kernels: none -> 121 us  [layer(): pl.pallas_call(kernel, out_shape=jax.ShapeDtypeStruct((T, D), bf16), in_s...]
    dot_general x7 -> x0, matrix products: 121 us -> none  [einsum(): return jnp.einsum(form, a.astype(jnp.float32), b.astype(jnp.float32))]
    another operation x1 -> x0, blocking collectives: 52.2 us -> none  [placed(): return lax.with_sharding_constraint(v, NamedSharding(mesh, P(*spec)))]
    another operation x1 -> x0, waiting for transfers between devices: 39.4 us -> none  [placed(): return lax.with_sharding_constraint(v, NamedSharding(mesh, P(*spec)))]
    another operation x4 -> x0, local copies, waits for them, and re-layouts: 11.3 us -> none  [placed(): return lax.with_sharding_constraint(v, NamedSharding(mesh, P(*spec)))]
    another operation x1 -> x0, starting transfers between devices: 7.01 us -> none  [placed(): return lax.with_sharding_constraint(v, NamedSharding(mesh, P(*spec)))]
    unnamed x17 -> x1, local copies, waits for them, and re-layouts: 6.66 us -> 2.06 us
  transfers between devices with their start and end apart: 1 -> 0, of which waited for: 1 -> 0; matrix products, arithmetic and copies ran while one was open for 2% -> 0% of each run, Pallas kernels for 0% -> 0%
where the time goes in v1:
time: 124 us; the launch traced here: 123 us
  Pallas kernels  121 us (98%)
  local copies, waits for them, and re-layouts  2.06 us (2%)
    pallas_call x1, Pallas kernels, layer(): pl.pallas_call(kernel, out_shape=jax.ShapeDtypeStruct((T, D), bf16), in_s...  121 us

profile of v1, /device:TPU:0, one launch (start us, length us, event | category | flops | bytes accessed | tf_op | source)
XLA Modules:
  0.0 123.3 jit_solution(2814473899573355152)
XLA Ops:
  0.0 121.3 %moe.1 = bf16[256,1536]{1,0:T(8,128)(2,1)} custom-call(s32[2,256]{1,0:T(2,128)} %bitcast.13, s32[2,256]{1,0:T(2,128)} %bitcast.14, f32[2,256]{1,0:T(2,128)} %bitcast.15, bf16[256,1536]{1,0:T(8,128)(2,1)} %bitcast.12, bf16[2,1536,9216]{2,1,0:T(8,128)(2,1)} %wg.1, bf16[2,1536,9216]{2,1,0:T(8,128)(2,1)} %wu.1, bf16[2,9216,1536]{2,1,0:T(8,128)(2,1)} %wd.1), custom_call_target="tpu_custom_call" | custom-call | tf_op jit(solution)/shard_map/moe/pallas_call | solution.py:258
  121.3 2.1 %copy.9 = bf16[1,1,256,1536]{3,2,1,0:T(8,128)(2,1)} copy(bf16[1,1,256,1536]{3,2,1,0:T(8,128)(2,1)} %bitcast.11) | data formatting | bytes 1572864

commit v2 on v1

v2 whole, which is shorter than its diff:
```python
import functools

import jax
import jax.numpy as jnp
from jax import lax
from jax.experimental import pallas as pl
from jax.experimental.pallas import tpu as pltpu
from jax.sharding import PartitionSpec as P

MESH = pl.DeviceIdType.MESH
N = 16
C = 20
T, D, F = 256, 1536, 9216
NH = 3
KD = D // NH
QD = KD // 2
TF = 512
NJ = F // TF
NK = 9
GU, GW = 9, 9
NBUF = NJ
PER = NH * (NJ + NK)
ROWS = N * C


def swap(a, b, first):
    return jnp.where(first, a, pltpu.roll(b, C, 0)), jnp.where(first, pltpu.roll(a, C, 0), b)


def peer(me, k):
    y, z, c = me // 8, (me // 2) % 4, me % 2
    half = (z // 2 + (k // 8) + 1) % 2
    zz = half * 2 + (z + k // 2) % 2
    return ((y + (k // 4)) % 2) * 8 + zz * 2 + (c + k) % 2


def kernel(
    expert_ref, slot_ref, gate_ref, x_ref, wg, wu, wd, y_ref,
    send, recv, rsend, rrecv, zbuf, zl, acc, h, oacc, obuf, ct, wbuf,
    wsem, ssem, rsem, rssem, rrsem,
):
    dp, me = lax.axis_index("dp"), lax.axis_index("ep")
    dot = functools.partial(jnp.dot, preferred_element_type=jnp.float32)

    def fetch_up(e, part, j, s):
        rows, cols = pl.ds(part * KD, KD), pl.ds(j * TF, TF)
        pltpu.make_async_copy(wg.at[e, rows, cols], wbuf.at[s, 0], wsem.at[s, 0]).start()
        pltpu.make_async_copy(wu.at[e, rows, cols], wbuf.at[s, 1], wsem.at[s, 1]).start()

    def fetch_down(e, c, k, s):
        for q in range(2):
            rows, cols = pl.ds((k * 2 + q) * TF, TF), pl.ds(c * KD, KD)
            pltpu.make_async_copy(wd.at[e, rows, cols], wbuf.at[s, q], wsem.at[s, q]).start()

    def arrived(slots):
        for s in slots:
            for q in range(2):
                pltpu.make_async_copy(
                    wg.at[0, pl.ds(0, KD), pl.ds(0, TF)], wbuf.at[s, q], wsem.at[s, q]
                ).wait()

    barrier = pltpu.get_barrier_semaphore()

    @pl.loop(1, N)
    def _(k):
        pl.semaphore_signal(barrier, inc=1, device_id=(dp, (me + k) % N), device_id_type=MESH)

    @pl.loop(0, NBUF)
    def _(n):
        fetch_up(0, 0, n, n)

    key = jnp.where(slot_ref[...] < C, expert_ref[...] * C + slot_ref[...], -1)
    k0, k1 = key[0:1, :], key[1:2, :]
    gate = gate_ref[...].astype(jnp.bfloat16).astype(jnp.float32)
    row = lax.broadcasted_iota(jnp.int32, (2 * ROWS, T), 0)
    hit0, hit1 = k0 == row, k1 == row
    pick = (jnp.where(hit0, 1.0, 0.0) + jnp.where(hit1, 1.0, 0.0)).astype(jnp.bfloat16)
    weighted = jnp.where(hit0, gate[0:1, :], 0.0) + jnp.where(hit1, gate[1:2, :], 0.0)
    ct[...] = weighted.astype(jnp.bfloat16)
    first = lax.broadcasted_iota(jnp.int32, (2 * C, QD), 0) < C

    def dispatch(e, part, k):
        to = peer(me, k)
        return pltpu.make_async_remote_copy(
            send.at[e, part, to], recv.at[e, part, me], ssem.at[e, part, to], rsem.at[e, part, me],
            device_id=(dp, to), device_id_type=MESH,
        )

    def send_all(e, part):
        for i in range(N - 1):
            dispatch(e, part, i + i // 8).start()

    def receive(e, part):
        @pl.loop(0, N - 1)
        def _(i):
            src = (me + 1 + i) % N
            pltpu.make_async_remote_copy(
                send.at[e, part, src], recv.at[e, part, src], ssem.at[e, part, src], rsem.at[e, part, src],
                device_id=(dp, src), device_id_type=MESH,
            ).wait_recv()

    for part in range(NH):
        zbuf[...] = dot(pick, x_ref[:, part * KD : (part + 1) * KD])

        @pl.loop(0, N)
        def _(d):
            rows = pl.ds(pl.multiple_of(d * 2 * C, 8), 2 * C)
            a, b = swap(zbuf[rows, :QD], zbuf[rows, QD:], first)
            send[0, part, d] = a.astype(jnp.bfloat16)
            send[1, part, d] = b.astype(jnp.bfloat16)

        for e in range(2):
            recv[e, part, me] = send[e, part, me]

    pl.semaphore_wait(barrier, N - 1)
    for part in range(NH):
        send_all(0, part)

    def gathered(e, part):
        receive(e, part)

        if part == 1:

            @pl.when(e == 0)
            def _():
                for later in range(NH):
                    send_all(1, later)

        @pl.loop(0, N // 4)
        def _(p):
            blocks = [recv[e, part, 4 * p + i].astype(jnp.float32) for i in range(4)]
            l0, h0 = swap(blocks[0], blocks[1], first)
            l1, h1 = swap(blocks[2], blocks[3], first)
            rows = pl.ds(pl.multiple_of(p * 4 * C, 16), 4 * C)
            zl[rows, :QD] = jnp.concatenate([l0, l1], axis=0).astype(jnp.bfloat16)
            zl[rows, QD:] = jnp.concatenate([h0, h1], axis=0).astype(jnp.bfloat16)

    def back(e, c, k):
        to = peer(me, k)
        return pltpu.make_async_remote_copy(
            rsend.at[e, c, to], rrecv.at[e, c, me], rssem.at[e, c, to], rrsem.at[e, c, me],
            device_id=(dp, to), device_id_type=MESH,
        )

    @pl.loop(0, 2)
    def _(e):
        for part in range(NH):
            gathered(e, part)

            @pl.loop(0, NJ // GU)
            def _(t):
                n = e * PER + part * NJ + t * GU
                for w in range(0, GU, GW):
                    slots = [(n + w + i) % NBUF for i in range(GW)]
                    arrived(slots)
                    for i, s in enumerate(slots):
                        j = t * GU + w + i
                        g, u = dot(zl[...], wbuf[s, 0]), dot(zl[...], wbuf[s, 1])
                        if part > 0:
                            g, u = acc[j, 0] + g, acc[j, 1] + u
                        if part < NH - 1:
                            acc[j, 0], acc[j, 1] = g, u
                            fetch_up(e, part + 1, j, s)
                        else:
                            h[j] = (g * jax.nn.sigmoid(g) * u).astype(jnp.bfloat16)
                            fetch_down(e, j // NK, j % NK, s)

        for c in range(NH):
            n = e * PER + NH * NJ + c * NK
            total = None
            for w in range(0, NK, GW):
                slots = [(n + w + i) % NBUF for i in range(GW)]
                arrived(slots)
                left = jnp.concatenate([h[2 * w + i] for i in range(2 * GW)], axis=1)
                right = jnp.concatenate([wbuf[s, q] for s in slots for q in range(2)], axis=0)
                more = dot(left, right)
                total = more if total is None else total + more
                for i, s in enumerate(slots):
                    if c == 0:
                        fetch_down(e, 2, w + i, s)
                    else:
                        fetch_up((e + 1) % 2, 0, (c - 1) * NK + w + i, s)
            oacc[...] = total

            @pl.loop(0, N // 2)
            def _(p):
                rows = pl.ds(pl.multiple_of(p * 2 * C, 8), 2 * C)
                a, b = swap(oacc[rows, :QD], oacc[rows, QD:], first)
                rsend[e, c, 2 * p] = a.astype(jnp.bfloat16)
                rsend[e, c, 2 * p + 1] = b.astype(jnp.bfloat16)

            for i in range(N - 1):
                back(e, c, i + i // 8).start()

            rrecv[e, c, me] = rsend[e, c, me]

    @pl.loop(0, NBUF)
    def _(s):
        arrived([s])

    def sent(copies):
        @pl.loop(0, N - 1)
        def _(i):
            to = (me + 1 + i) % N
            for src, sem, e, part in copies:
                pltpu.make_async_remote_copy(
                    src.at[e, part, to], src.at[e, part, to], sem.at[e, part, to], rsem.at[e, part, to],
                    device_id=(dp, to), device_id_type=MESH,
                ).wait_send()

    sent([(send, ssem, e, part) for e in range(2) for part in range(NH)])
    sent([(rsend, rssem, 0, part) for part in range(NH)])

    for c in range(NH):
        @pl.loop(0, N - 1)
        def _(i):
            src = (me + 1 + i) % N
            for e in range(2):
                pltpu.make_async_remote_copy(
                    rsend.at[e, c, src], rrecv.at[e, c, src], rssem.at[e, c, src], rrsem.at[e, c, src],
                    device_id=(dp, src), device_id_type=MESH,
                ).wait_recv()

        @pl.loop(0, N // 2)
        def _(p):
            parts = [
                swap(rrecv[0, c, 2 * p + i].astype(jnp.float32), rrecv[1, c, 2 * p + i].astype(jnp.float32), first)
                for i in range(2)
            ]
            rows = pl.ds(pl.multiple_of(p * 4 * C, 16), 4 * C)
            for i in range(2):
                obuf[rows, i * QD : (i + 1) * QD] = jnp.concatenate(
                    [parts[0][i], parts[1][i]], axis=0
                ).astype(jnp.bfloat16)

        sent([(rsend, rssem, 1, c)])
        y_ref[:, c * KD : (c + 1) * KD] = lax.dot_general(
            ct[...], obuf[...], (((0,), (0,)), ((), ())), preferred_element_type=jnp.float32
        ).astype(jnp.bfloat16)


def solution(mesh):
    spec = P("dp", "ep")

    def layer(x, expert, slot, gate, w_gate, w_up, w_down):
        vmem = pl.BlockSpec(memory_space=pltpu.VMEM)
        hbm = pl.BlockSpec(memory_space=pl.ANY)
        bf16, f32 = jnp.bfloat16, jnp.float32
        dma = pltpu.SemaphoreType.DMA
        y = pl.pallas_call(
            kernel,
            out_shape=jax.ShapeDtypeStruct((T, D), bf16),
            in_specs=[vmem] * 4 + [hbm] * 3,
            out_specs=vmem,
            scratch_shapes=[
                pltpu.VMEM((2, NH, N, 2 * C, QD), bf16),
                pltpu.VMEM((2, NH, N, 2 * C, QD), bf16),
                pltpu.VMEM((2, NH, N, 2 * C, QD), bf16),
                pltpu.VMEM((2, NH, N, 2 * C, QD), bf16),
                pltpu.VMEM((2 * ROWS, KD), f32),
                pltpu.VMEM((ROWS, KD), bf16),
                pltpu.VMEM((NJ, 2, ROWS, TF), f32),
                pltpu.VMEM((NJ, ROWS, TF), bf16),
                pltpu.VMEM((ROWS, KD), f32),
                pltpu.VMEM((2 * ROWS, KD), bf16),
                pltpu.VMEM((2 * ROWS, T), bf16),
                pltpu.VMEM((NBUF, 2, KD, TF), bf16),
                dma((NBUF, 2)),
                dma((2, NH, N)),
                dma((2, NH, N)),
                dma((2, NH, N)),
                dma((2, NH, N)),
            ],
            compiler_params=pltpu.CompilerParams(
                collective_id=0, has_side_effects=True, vmem_limit_bytes=67_000_000
            ),
            name="moe",
        )(
            expert.reshape(T, 2).T, slot.reshape(T, 2).T, gate.reshape(T, 2).T,
            x.reshape(T, D), w_gate, w_up, w_down,
        )
        return y.reshape(1, 1, T, D)

    return jax.shard_map(
        layer, mesh=mesh,
        in_specs=(spec, spec, spec, spec, P("ep"), P("ep"), P("ep")),
        out_specs=spec, check_vma=False,
    )
```

time: 124 us -> 107 us (0.86)
  Pallas kernels: 121 us -> 105 us
    pallas_call x1, Pallas kernels: 121 us -> 105 us  [layer(): pl.pallas_call(kernel, out_shape=jax.ShapeDtypeStruct((T, D), bf16), in_s...]
where the time goes in v2:
time: 107 us
  Pallas kernels  105 us (98%)
  local copies, waits for them, and re-layouts  2.06 us (2%)
    pallas_call x1, Pallas kernels, layer(): pl.pallas_call(kernel, out_shape=jax.ShapeDtypeStruct((T, D), bf16), in_s...  105 us

profile of v2, /device:TPU:0, one launch (start us, length us, event | category | flops | bytes accessed | tf_op | source)
XLA Modules:
  0.0 107.0 jit_solution(10944007940195819156)
XLA Ops:
  0.0 105.0 %moe.1 = bf16[256,1536]{1,0:T(8,128)(2,1)} custom-call(s32[2,256]{1,0:T(2,128)} %bitcast.13, s32[2,256]{1,0:T(2,128)} %bitcast.14, f32[2,256]{1,0:T(2,128)} %bitcast.15, bf16[256,1536]{1,0:T(8,128)(2,1)} %bitcast.12, bf16[2,1536,9216]{2,1,0:T(8,128)(2,1)} %wg.1, bf16[2,1536,9216]{2,1,0:T(8,128)(2,1)} %wu.1, bf16[2,9216,1536]{2,1,0:T(8,128)(2,1)} %wd.1), custom_call_target="tpu_custom_call" | custom-call | tf_op jit(solution)/shard_map/moe/pallas_call | solution.py:250
  105.0 2.1 %copy.9 = bf16[1,1,256,1536]{3,2,1,0:T(8,128)(2,1)} copy(bf16[1,1,256,1536]{3,2,1,0:T(8,128)(2,1)} %bitcast.11) | data formatting | bytes 1572864
